TPU v7x, 32 devices: a whole 2x2x4 slice. The times are simulated.
32 devices in a mesh: cell: 8 (over z, x), seq: 4 (over y, core).
Axes of the slice: x: 2, y: 2, z: 4, core: 2. Of those that a mesh axis runs over, the one named last changes fastest.
Arguments:
- cells_in: bfloat16 [8, 1024, 1120], P('cell', 'seq'), may hold values from -6 to 6
- dataset_ids: int32 [8], P('cell'), may hold values from 0 to 15
- cell_lengths: int32 [8], P('cell'), may hold values from 512 to 1024, as said below
- table: float32 [16, 1120], replicated, may hold values from -3 to 3
- wqkv: bfloat16 [1120, 3360], P('seq'), may hold values from -0.25 to 0.25
- bq: float32 [1120], replicated, may hold values from -3 to 3
- bv: float32 [1120], replicated, may hold values from -3 to 3
- wout: bfloat16 [1120, 1120], P('seq'), may hold values from -0.5 to 0.5
- bout: float32 [1120], replicated, may hold values from -2 to 2
- gain1: float32 [1120], replicated, may hold values from 0.1 to 1.9
- shift1: float32 [1120], replicated, may hold values from -2 to 2
- gain2: float32 [1120], replicated, may hold values from 0.1 to 1.9
- shift2: float32 [1120], replicated, may hold values from -2 to 2
- wup: bfloat16 [1120, 4480], P(None, 'cell'), may hold values from -0.1875 to 0.1875
- bup: float32 [4480], replicated, may hold values from -2 to 2
- wdown: bfloat16 [4480, 1120], P('cell'), may hold values from -0.09375 to 0.09375
- bdown: float32 [1120], replicated, may hold values from -2 to 2
- out_grad: bfloat16 [8, 1024, 1120], P('cell', 'seq'), may hold values from -6 to 6
Outputs:
- cells_out: bfloat16 [8, 1024, 1120], P('cell', 'seq')
- cells_grad: bfloat16 [8, 1024, 1120], P('cell', 'seq')
- grad_table: float32 [16, 1120], P(None, 'seq')
- grad_wqkv: float32 [1120, 3360], P('seq')
- grad_bq: float32 [1120], P('seq')
- grad_bv: float32 [1120], P('seq')
- grad_wout: float32 [1120, 1120], P('seq')
- grad_bout: float32 [1120], P('seq')
- grad_gain1: float32 [1120], P('seq')
- grad_shift1: float32 [1120], P('seq')
- grad_gain2: float32 [1120], P('seq')
- grad_shift2: float32 [1120], P('seq')
- grad_wup: float32 [1120, 4480], P(None, 'cell')
- grad_bup: float32 [4480], P('seq')
- grad_wdown: float32 [4480, 1120], P('cell')
- grad_bdown: float32 [1120], P('seq')
Inputs may be any that keep to these rules, and one draw needn't show every extreme that they name: `cell_lengths`: some cell has exactly 1024 live positions.
All inputs are finite; a program needn't handle non-finite values.
Results may differ from a plain program's by a relative error of at most 0.015.
Values may be sent and summed in bfloat16 or wider, within the bound.
A program may use at most 256 MiB of HBM per device.

v0:
```python
import math

import jax
import jax.numpy as jnp
from jax import lax
from jax.sharding import PartitionSpec as P

HEAD_DIM = 56


norm_eps = 1e-05


def cut_along(x, dim, size):
    lengths = x.shape
    parts = x.reshape(*lengths[:dim], size, lengths[dim] // size, *lengths[dim + 1 :])
    return jnp.moveaxis(parts, dim, 0)


def sent_and_summed(x, axis, dim):
    parts = cut_along(x, dim, lax.axis_size(axis))
    arrived = lax.all_to_all(parts, axis, split_axis=0, concat_axis=0, tiled=True)
    return arrived.astype(jnp.float32).sum(axis=0)


def product(left, right):
    return jnp.dot(left, right, preferred_element_type=jnp.float32)


def left_inner(left, right):
    return lax.dot_general(
        left, right, (((0,), (0,)), ((), ())), preferred_element_type=jnp.float32
    )


def right_inner(left, right):
    return lax.dot_general(
        left, right, (((1,), (1,)), ((), ())), preferred_element_type=jnp.float32
    )


def norm_forward(hidden, gain, shift):
    centre = hidden - jnp.mean(hidden, axis=-1, keepdims=True)
    inverse = lax.rsqrt(jnp.mean(centre * centre, axis=-1, keepdims=True) + norm_eps)
    unit_rows = centre * inverse
    return (unit_rows * gain + shift, unit_rows, inverse)


def norm_backward(grad_rows, unit_rows, inverse, gain):
    scaled = grad_rows * gain
    inside = (
        scaled
        - jnp.mean(scaled, axis=-1, keepdims=True)
        - unit_rows * jnp.mean(scaled * unit_rows, axis=-1, keepdims=True)
    )
    return (inside * inverse, jnp.sum(grad_rows * unit_rows, axis=0), jnp.sum(grad_rows, axis=0))


def block_scores(queries, keys_used, first_row, length, score_scale):
    row_count = queries.shape[0]
    key_count = keys_used.shape[0]
    scores = (
        jnp.einsum("qhd,khd->hqk", queries, keys_used, preferred_element_type=jnp.float32)
        * score_scale
    )
    query_pos = first_row + lax.broadcasted_iota(jnp.int32, (row_count, key_count), 0)
    key_pos = lax.broadcasted_iota(jnp.int32, (row_count, key_count), 1)
    visible = (key_pos <= query_pos) & (key_pos < length)
    return jnp.where(visible[None], scores, -1e30)


def attend_forward(query_heads, key_heads, value_heads, length, row_block, score_scale):
    slot_count = query_heads.shape[0]
    outputs = []
    logsums = []
    for block_idx in range(slot_count // row_block):
        first_row = block_idx * row_block
        key_count = first_row + row_block
        scores = block_scores(
            query_heads[first_row:key_count], key_heads[:key_count], first_row, length, score_scale
        )
        highest = jnp.max(scores, axis=-1, keepdims=True)
        weights = jnp.exp(scores - highest)
        denominator = jnp.sum(weights, axis=-1, keepdims=True)
        prob_low = (weights / denominator).astype(jnp.bfloat16)
        outputs.append(
            jnp.einsum(
                "hqk,khd->qhd",
                prob_low,
                value_heads[:key_count],
                preferred_element_type=jnp.float32,
            )
        )
        logsums.append(highest + jnp.log(denominator))
    return (jnp.concatenate(outputs, axis=0), logsums)


def attend_backward(
    query_heads, key_heads, value_heads, grad_heads, logsums, length, row_block, score_scale
):
    slot_count = query_heads.shape[0]
    grad_query = []
    grad_key = jnp.zeros(key_heads.shape, jnp.float32)
    grad_value = jnp.zeros(value_heads.shape, jnp.float32)
    for block_idx in range(slot_count // row_block):
        first_row = block_idx * row_block
        key_count = first_row + row_block
        queries = query_heads[first_row:key_count]
        grads_here = grad_heads[first_row:key_count]
        scores = block_scores(queries, key_heads[:key_count], first_row, length, score_scale)
        prob_full = jnp.exp(scores - logsums[block_idx])
        prob_low = prob_full.astype(jnp.bfloat16)
        grad_prob = jnp.einsum(
            "qhd,khd->hqk", grads_here, value_heads[:key_count], preferred_element_type=jnp.float32
        )
        grad_value = grad_value.at[:key_count].add(
            jnp.einsum("hqk,qhd->khd", prob_low, grads_here, preferred_element_type=jnp.float32)
        )
        row_inner = jnp.sum(prob_full * grad_prob, axis=-1, keepdims=True)
        grad_score = (prob_full * (grad_prob - row_inner)).astype(jnp.bfloat16)
        grad_query.append(
            jnp.einsum(
                "hqk,khd->qhd",
                grad_score,
                key_heads[:key_count],
                preferred_element_type=jnp.float32,
            )
            * score_scale
        )
        grad_key = grad_key.at[:key_count].add(
            jnp.einsum("hqk,qhd->khd", grad_score, queries, preferred_element_type=jnp.float32)
            * score_scale
        )
    return (jnp.concatenate(grad_query, axis=0), grad_key, grad_value)


def shards(
    cells_in,
    dataset_ids,
    cell_lengths,
    table,
    wqkv,
    bq,
    bv,
    wout,
    bout,
    gain1,
    shift1,
    gain2,
    shift2,
    wup,
    bup,
    wdown,
    bdown,
    out_grad,
):
    seq_count = lax.axis_size("seq")
    local_rows = cells_in.shape[1]
    width = cells_in.shape[2]
    slot_count = local_rows * seq_count
    group_width = width // seq_count
    heads_here = group_width // HEAD_DIM
    row_block = min(512, slot_count)
    score_scale = 1.0 / math.sqrt(HEAD_DIM)
    length = cell_lengths[0]
    dataset_pick = (
        lax.broadcasted_iota(jnp.int32, (1, table.shape[0]), 1) == dataset_ids[0]
    ).astype(jnp.float32)
    table_row = jnp.dot(
        dataset_pick, table, precision=lax.Precision.HIGHEST, preferred_element_type=jnp.float32
    )
    resid_in = cells_in[0].astype(jnp.float32) + table_row
    normed1, unit1, inverse1 = norm_forward(resid_in, gain1, shift1)
    normed1_low = normed1.astype(jnp.bfloat16)
    wqkv_full, wout_full = (
        lax.all_gather(wqkv, "seq", axis=0, tiled=True),
        lax.all_gather(wout, "seq", axis=0, tiled=True),
    )
    qkv_bias = jnp.concatenate([bq, jnp.zeros_like(bq), bv])
    qkv_low = (product(normed1_low, wqkv_full) + qkv_bias).astype(jnp.bfloat16)
    qkv_heads = lax.all_to_all(
        qkv_low.reshape(local_rows, 3, seq_count, group_width),
        "seq",
        split_axis=2,
        concat_axis=0,
        tiled=True,
    )
    query_heads = qkv_heads[:, 0, 0].reshape(slot_count, heads_here, HEAD_DIM)
    key_heads = qkv_heads[:, 1, 0].reshape(slot_count, heads_here, HEAD_DIM)
    value_heads = qkv_heads[:, 2, 0].reshape(slot_count, heads_here, HEAD_DIM)
    context, logsums = attend_forward(
        query_heads, key_heads, value_heads, length, row_block, score_scale
    )
    context_low = context.astype(jnp.bfloat16).reshape(slot_count, 1, group_width)
    context_rows = lax.all_to_all(
        context_low, "seq", split_axis=0, concat_axis=1, tiled=True
    ).reshape(local_rows, width)
    resid_mid = resid_in + product(context_rows, wout_full) + bout
    normed2, unit2, inverse2 = norm_forward(resid_mid, gain2, shift2)
    normed2_low = normed2.astype(jnp.bfloat16)
    wup_full, wdown_full = (
        lax.all_gather(wup, "cell", axis=1, tiled=True),
        lax.all_gather(wdown, "cell", axis=0, tiled=True),
    )
    up_rows = product(normed2_low, wup_full) + bup
    act_low = jax.nn.gelu(up_rows, approximate=True).astype(jnp.bfloat16)
    cells_out = (resid_mid + product(act_low, wdown_full) + bdown).astype(jnp.bfloat16)[None]
    grad_out = out_grad[0]
    grad_rows = grad_out.astype(jnp.float32)
    grad_bdown = jnp.sum(grad_rows, axis=0)
    grad_wdown = left_inner(act_low, grad_out)
    wup_back, wdown_back = (
        lax.all_gather(wup, "cell", axis=1, tiled=True),
        lax.all_gather(wdown, "cell", axis=0, tiled=True),
    )
    grad_act = right_inner(grad_out, wdown_back)
    gelu_pull = jax.vjp(lambda values: jax.nn.gelu(values, approximate=True), up_rows)[1]
    grad_up_low = gelu_pull(grad_act)[0].astype(jnp.bfloat16)
    grad_bup = jnp.sum(grad_up_low.astype(jnp.float32), axis=0)
    grad_wup = left_inner(normed2_low, grad_up_low)
    grad_norm2 = right_inner(grad_up_low, wup_back)
    back_second, grad_gain2, grad_shift2 = norm_backward(grad_norm2, unit2, inverse2, gain2)
    grad_mid = grad_rows + back_second
    grad_mid_low = grad_mid.astype(jnp.bfloat16)
    grad_bout = jnp.sum(grad_mid_low.astype(jnp.float32), axis=0)
    grad_context = right_inner(grad_mid_low, wout_full).astype(jnp.bfloat16)
    grad_context_heads = lax.all_to_all(
        grad_context.reshape(local_rows, seq_count, group_width),
        "seq",
        split_axis=1,
        concat_axis=0,
        tiled=True,
    ).reshape(slot_count, heads_here, HEAD_DIM)
    grad_query, grad_key, grad_value = attend_backward(
        query_heads,
        key_heads,
        value_heads,
        grad_context_heads,
        logsums,
        length,
        row_block,
        score_scale,
    )
    grad_qkv_heads = jnp.stack([grad_query, grad_key, grad_value], axis=1).astype(jnp.bfloat16)
    grad_qkv = lax.all_to_all(
        grad_qkv_heads.reshape(slot_count, 3, 1, group_width),
        "seq",
        split_axis=0,
        concat_axis=2,
        tiled=True,
    ).reshape(local_rows, 3 * width)
    grad_qkv_wide = grad_qkv.astype(jnp.float32)
    grad_bq = jnp.sum(grad_qkv_wide[:, :width], axis=0)
    grad_bv = jnp.sum(grad_qkv_wide[:, 2 * width :], axis=0)
    grad_norm1 = right_inner(grad_qkv, wqkv_full)
    back_first, grad_gain1, grad_shift1 = norm_backward(grad_norm1, unit1, inverse1, gain1)
    grad_in = grad_mid + back_first
    cells_grad = grad_in.astype(jnp.bfloat16)[None]
    grad_table = jnp.transpose(dataset_pick) * jnp.sum(grad_in, axis=0)[None, :]
    grad_wqkv = left_inner(normed1_low, grad_qkv)
    grad_wout = left_inner(context_rows, grad_mid_low)
    seq_parts = (
        lax.psum_scatter(
            grad_table.astype(jnp.bfloat16), "seq", scatter_dimension=1, tiled=True
        ).astype(jnp.float32),
        lax.psum_scatter(
            grad_wqkv.astype(jnp.bfloat16), "seq", scatter_dimension=0, tiled=True
        ).astype(jnp.float32),
        lax.psum_scatter(
            grad_wout.astype(jnp.bfloat16), "seq", scatter_dimension=0, tiled=True
        ).astype(jnp.float32),
        lax.psum_scatter(
            grad_bq.astype(jnp.bfloat16), "seq", scatter_dimension=0, tiled=True
        ).astype(jnp.float32),
        lax.psum_scatter(
            grad_bv.astype(jnp.bfloat16), "seq", scatter_dimension=0, tiled=True
        ).astype(jnp.float32),
        lax.psum_scatter(
            grad_bout.astype(jnp.bfloat16), "seq", scatter_dimension=0, tiled=True
        ).astype(jnp.float32),
        lax.psum_scatter(
            grad_gain1.astype(jnp.bfloat16), "seq", scatter_dimension=0, tiled=True
        ).astype(jnp.float32),
        lax.psum_scatter(
            grad_shift1.astype(jnp.bfloat16), "seq", scatter_dimension=0, tiled=True
        ).astype(jnp.float32),
        lax.psum_scatter(
            grad_gain2.astype(jnp.bfloat16), "seq", scatter_dimension=0, tiled=True
        ).astype(jnp.float32),
        lax.psum_scatter(
            grad_shift2.astype(jnp.bfloat16), "seq", scatter_dimension=0, tiled=True
        ).astype(jnp.float32),
        lax.psum_scatter(
            grad_bup.astype(jnp.bfloat16), "seq", scatter_dimension=0, tiled=True
        ).astype(jnp.float32),
        lax.psum_scatter(
            grad_bdown.astype(jnp.bfloat16), "seq", scatter_dimension=0, tiled=True
        ).astype(jnp.float32),
    )
    share_qkv = seq_parts[1]
    share_out = seq_parts[2]
    part_qkv, part_out = (
        sent_and_summed(share_qkv.reshape(-1).astype(jnp.bfloat16), "cell", 0),
        sent_and_summed(share_out.reshape(-1).astype(jnp.bfloat16), "cell", 0),
    )
    whole_qkv, whole_out = (
        lax.all_gather(part_qkv.astype(jnp.bfloat16), "cell", axis=0, tiled=True).astype(
            part_qkv.dtype
        ),
        lax.all_gather(part_out.astype(jnp.bfloat16), "cell", axis=0, tiled=True).astype(
            part_out.dtype
        ),
    )
    total_wqkv = whole_qkv.reshape(share_qkv.shape)
    total_wout = whole_out.reshape(share_out.shape)
    others = lax.psum((seq_parts[0],) + tuple(seq_parts[3:]), "cell")
    summed = (others[0], total_wqkv, total_wout) + tuple(others[1:])
    cell_up, cell_down = (
        lax.psum_scatter(grad_wup, "cell", scatter_dimension=1, tiled=True),
        lax.psum_scatter(grad_wdown, "cell", scatter_dimension=0, tiled=True),
    )
    total_up, total_down = (
        lax.psum(cell_up.astype(jnp.bfloat16), "seq").astype(jnp.float32),
        lax.psum(cell_down.astype(jnp.bfloat16), "seq").astype(jnp.float32),
    )
    return (
        cells_out,
        cells_grad,
        summed[0],
        summed[1],
        summed[3],
        summed[4],
        summed[2],
        summed[5],
        summed[6],
        summed[7],
        summed[8],
        summed[9],
        total_up,
        summed[10],
        total_down,
        summed[11],
    )


def solution(mesh):
    return jax.shard_map(
        shards,
        mesh=mesh,
        in_specs=(
            P("cell", "seq", None),
            P("cell"),
            P("cell"),
            P(),
            P("seq", None),
            P(),
            P(),
            P("seq", None),
            P(),
            P(),
            P(),
            P(),
            P(),
            P(None, "cell"),
            P(),
            P("cell", None),
            P(),
            P("cell", "seq", None),
        ),
        out_specs=(
            P("cell", "seq", None),
            P("cell", "seq", None),
            P(None, "seq"),
            P("seq", None),
            P("seq"),
            P("seq"),
            P("seq", None),
            P("seq"),
            P("seq"),
            P("seq"),
            P("seq"),
            P("seq"),
            P(None, "cell"),
            P("seq"),
            P("cell", None),
            P("seq"),
        ),
        check_vma=False,
    )
```

profile of v0, /device:TPU:0, one launch (start us, length us, event | category | flops | bytes accessed | tf_op | source)
XLA Modules:
  0.0 1535.3 jit_solution(6749002238563494380)
XLA Ops:
  11.5 55.4 %all-gather.5.cloned.1.call-done = bf16[1120,3360]{1,0:T(8,128)(2,1)} async-done(((bf16[280,3360]{1,0:T(8,128)(2,1)}), bf16[1120,3360]{1,0:T(8,128)(2,1)}) %all-gather.5.cloned.1.call-update) | async-done | bytes 7526416 | tf_op jit(solution)/shard_map/all_gather | solution.py:176
  67.0 7.2 fusion.6
  81.6 29.2 %all-to-all-done = bf16[256,3,4,280]{0,3,1,2:T(8,128)(2,1)S(1)} async-done(((bf16[256,3,4,280]{0,3,1,2:T(8,128)(2,1)}), bf16[256,3,4,280]{0,3,1,2:T(8,128)(2,1)S(1)}, u32[]{:S(2)}, u32[]{:S(2)}) %all-to-all-start) | async-done | bytes 1720352 | tf_op jit(solution)/shard_map/all_to_all | solution.py:181
  131.0 9.3 all-to-all-done.1
  148.6 105.9 %all-gather.9.cloned.1.call-done = bf16[1120,4480]{0,1:T(8,128)(2,1)} async-done(((bf16[1120,560]{0,1:T(8,128)(2,1)}), bf16[1120,4480]{0,1:T(8,128)(2,1)}) %all-gather.9.cloned.1.call-update) | async-done | bytes 10035216 | tf_op jit(solution)/shard_map/all_gather | solution.py:202
  254.4 9.8 convolution_add_fusion
  264.2 138.9 %all-gather.11.cloned.1.call-done = bf16[4480,1120]{1,0:T(8,128)(2,1)} async-done(((bf16[560,1120]{1,0:T(8,128)(2,1)}), bf16[4480,1120]{1,0:T(8,128)(2,1)}) %all-gather.11.cloned.1.call-update) | async-done | bytes 10035216 | tf_op jit(solution)/shard_map/all_gather | solution.py:203
  403.2 12.5 fusion.104
  415.7 10.0 multiply_reduce_fusion.2
  496.2 7.6 pad_maximum_fusion
  503.8 39.4 %all_to_all.75 = bf16[1024,3,1,280]{3,1,2,0:T(4,128)(2,1)S(1)} all-to-all(bf16[1024,3,1,280]{3,1,2,0:T(4,128)(2,1)S(1)} %pad_maximum_fusion), channel_id=1, replica_groups=mesh['cell'=8,'seq'=4] {'seq'}, dimensions={0} | all-to-all | bytes 3440640 | tf_op jit(solution)/shard_map/all_to_all | solution.py:245
  555.1 14.6 fusion.95
  569.7 13.7 fusion.73
  600.3 20.8 %reduce-scatter.14.cloned.1.call-done = bf16[280,3360]{1,0:T(8,128)(2,1)} async-done(((bf16[1120,3360]{1,0:T(8,128)(2,1)}), bf16[280,3360]{1,0:T(8,128)(2,1)}) %reduce-scatter.14.cloned.1.call-update) | async-done | bytes 1881616
  632.1 42.0 %reduce.19 = bf16[8,117600]{1,0:T(8,128)(2,1)} reduce(bf16[8,1,117600]{2,1,0:T(2,128)(2,1)} %convert_element_type.245, bf16[]{:T(256)} %broadcast.342), dimensions={1}, to_apply=%convert_element_type.245.reduce_sub_computation | reduce | bytes 3763202 | tf_op jit(solution)/shard_map/convert_element_type | solution.py:303
  700.3 73.3 %all-to-all-done.4 = bf16[8,2,58800]{2,1,0:T(2,128)(2,1)} async-done(((bf16[8,2,58800]{2,1,0:T(2,128)(2,1)}), bf16[8,2,58800]{2,1,0:T(2,128)(2,1)}, u32[]{:S(2)}, u32[]{:S(2)}) %all-to-all-start.4) | async-done | bytes 1881632 | tf_op jit(solution)/shard_map/all_to_all | solution.py:22
  773.6 7.9 reshape.517
  794.4 11.3 fusion.23
  815.2 188.4 %reduce-scatter.10.cloned.1.call-done = f32[1120,560]{0,1:T(8,128)} async-done(((f32[1120,4480]{0,1:T(8,128)}), f32[1120,560]{0,1:T(8,128)}) %reduce-scatter.10.cloned.1.call-update) | async-done | bytes 2508816 | tf_op jit(solution)/shard_map/reduce_scatter | solution.py:319
  1006.5 337.0 %reduce-scatter.12.cloned.1.call-done = f32[560,1120]{1,0:T(8,128)} async-done(((f32[4480,1120]{1,0:T(8,128)}), f32[560,1120]{1,0:T(8,128)}) %reduce-scatter.12.cloned.1.call-update) | async-done | bytes 2508816 | tf_op jit(solution)/shard_map/reduce_scatter | solution.py:320
  1347.2 12.6 all-reduce.18
  1360.6 38.1 %all-reduce.16 = (f32[16,280]{1,0:T(8,128)}, f32[280]{0:T(512)}, f32[280]{0:T(512)}, f32[280]{0:T(512)}, f32[280]{0:T(512)}, /*index=5*/f32[280]{0:T(512)}, f32[...) all-reduce(f32[16,280]{1,0:T(8,128)S(1)} %dynamic-slice_convert_fus, ...), channel_id=1, replica_groups=mesh['cell'=8,'seq'=4] {'cell'}, use_global_device_ids=true, to_apply=%region_16.17 | all-reduce | flops 7840 | bytes 62720 | tf_op jit(solution)/shard_map/psum | solution.py:316
  1398.7 63.3 %all-reduce.23.cloned.1.call-done = (bf16[940800]{0:T(1024)(128)(2,1)}, bf16[313600]{0:T(1024)(128)(2,1)}) async-done(((bf16[940800]{0:T(1024)(128)(2,1)}, bf16[313600]{0:T(1024)(128)(2,1)}), (bf16[940800]{0:T(1024)(128)(2,1)}, bf16[313600]{0:T(1024)(128)(2,1)})) %all-reduce.23.cloned.1.call-update) | async-done | bytes 2508816
  1469.4 54.1 %all-reduce.25.cloned.1.call-done = (bf16[1120,560]{0,1:T(8,128)(2,1)}, bf16[560,1120]{1,0:T(8,128)(2,1)}) async-done(((bf16[1120,560]{0,1:T(8,128)(2,1)}, bf16[560,1120]{1,0:T(8,128)(2,1)}), (bf16[1120,560]{0,1:T(8,128)(2,1)}, bf16[560,1120]{1,0:T(8,128)(2,1)})) %all-reduce.25.cloned.1.call-update) | async-done | bytes 2508816 | tf_op jit(solution)/shard_map/psum | solution.py:323
  (245 shorter events, 213.7 us)
Async XLA Ops:
  7.2 59.7 %all-gather.5.cloned.1.call-start = ((), (), s32[]{:S(2)}) async-start(), calls=%async_computation.10 | async-start | bytes 9676800 | tf_op jit(solution)/shard_map/all_gather | solution.py:176
  8.0 59.0 %copy-start.35 = (f32[1120]{0:T(1024)S(1)}, f32[1120]{0:T(1024)}, u32[]{:S(2)}) copy-start(f32[1120]{0:T(1024)} %param.39) | copy-start | bytes 13444
  8.0 137.0 %all-gather.7.cloned.1.call-start = ((), (), s32[]{:S(2)}) async-start(), calls=%async_computation.11 | async-start | bytes 3225600 | tf_op jit(solution)/shard_map/all_gather | solution.py:177
  8.7 245.7 %all-gather.9.cloned.1.call-start = ((), (), s32[]{:S(2)}) async-start(), calls=%async_computation.12 | async-start | bytes 11612160 | tf_op jit(solution)/shard_map/all_gather | solution.py:202
  9.5 393.7 %all-gather.11.cloned.1.call-start = ((), (), s32[]{:S(2)}) async-start(), calls=%async_computation.13 | async-start | bytes 11612160 | tf_op jit(solution)/shard_map/all_gather | solution.py:203
  11.5 62.7 %copy-start.39 = (f32[256]{0:T(256)}, f32[256]{0:T(256)S(1)}, u32[]{:S(2)}) copy-start(f32[256]{0:T(256)S(1)} %add_rsqrt_fusion.1) | copy-start | bytes 3076
  75.5 35.3 %all-to-all-start = ((bf16[256,3,4,280]{0,3,1,2:T(8,128)(2,1)}), bf16[256,3,4,280]{0,3,1,2:T(8,128)(2,1)S(1)}, u32[]{:S(2)}, u32[]{:S(2)}) async-start(bf16[256,3,4,280]{0,3,1,2:T(8,128)(2,1)} %copy.78), calls=%async_computation | async-start | bytes 3440640 | tf_op jit(solution)/shard_map/all_to_all | solution.py:181
  127.3 12.9 all-to-all-start.1
  145.0 109.5 %copy-start.33 = (f32[1120]{0:T(1024)S(1)}, f32[1120]{0:T(1024)}, u32[]{:S(2)}) copy-start(f32[1120]{0:T(1024)} %param.41) | copy-start | bytes 13444
  145.0 109.4 %copy-start.34 = (f32[1120]{0:T(1024)S(1)}, f32[1120]{0:T(1024)}, u32[]{:S(2)}) copy-start(f32[1120]{0:T(1024)} %param.42) | copy-start | bytes 13444
  145.0 109.4 %copy-start.48 = (f32[4480]{0:T(1024)S(1)}, f32[4480]{0:T(1024)}, u32[]{:S(2)}) copy-start(f32[4480]{0:T(1024)} %param.44) | copy-start | bytes 53764
  148.3 277.5 %copy-start.7 = (f32[256,1120]{0,1:T(8,128)}, f32[256,1120]{0,1:T(8,128)S(1)}, u32[]{:S(2)}) copy-start(f32[256,1120]{0,1:T(8,128)S(1)} %get-tuple-element.131) | copy-start | bytes 3440644
  148.5 277.3 %copy-start.37 = (f32[256]{0:T(256)}, f32[256]{0:T(256)S(1)}, u32[]{:S(2)}) copy-start(f32[256]{0:T(256)S(1)} %add_rsqrt_fusion) | copy-start | bytes 3076
  148.5 254.6 %copy-start.14 = (bf16[1,256,1120]{1,2,0:T(8,128)(2,1)S(1)}, bf16[1,256,1120]{1,2,0:T(8,128)(2,1)}, u32[]{:S(2)}) copy-start(bf16[1,256,1120]{1,2,0:T(8,128)(2,1)} %param.47) | copy-start | bytes 1720324
  429.3 12.8 all-to-all-start.2
  432.7 150.7 %reduce-scatter.16.cloned.1.call-start = ((), (), s32[]{:S(2)}) async-start(), calls=%async_computation.17 | async-start | bytes 3225600
  435.3 185.9 %reduce-scatter.14.cloned.1.call-start = ((), (), s32[]{:S(2)}) async-start(), calls=%async_computation.16 | async-start | bytes 9676800
  553.8 449.7 %reduce-scatter.10.cloned.1.call-start = ((), (), s32[]{:S(2)}) async-start(), calls=%async_computation.14 | async-start | bytes 23224320 | tf_op jit(solution)/shard_map/reduce_scatter | solution.py:319
  569.7 773.9 %reduce-scatter.12.cloned.1.call-start = ((), (), s32[]{:S(2)}) async-start(), calls=%async_computation.15 | async-start | bytes 23224320 | tf_op jit(solution)/shard_map/reduce_scatter | solution.py:320
  595.7 83.1 %all-to-all-start.5 = ((bf16[8,2,19600]{2,1,0:T(2,128)(2,1)}), bf16[8,2,19600]{2,1,0:T(2,128)(2,1)}, u32[]{:S(2)}, u32[]{:S(2)}) async-start(bf16[8,2,19600]{2,1,0:T(2,128)(2,1)} %reshape.518), calls=%async_computation.5 | async-start | bytes 1261568 | tf_op jit(solution)/shard_map/all_to_all | solution.py:22
  678.8 94.8 %all-to-all-start.4 = ((bf16[8,2,58800]{2,1,0:T(2,128)(2,1)}), bf16[8,2,58800]{2,1,0:T(2,128)(2,1)}, u32[]{:S(2)}, u32[]{:S(2)}) async-start(bf16[8,2,58800]{2,1,0:T(2,128)(2,1)} %reshape.516), calls=%async_computation.4 | async-start | bytes 3768320 | tf_op jit(solution)/shard_map/all_to_all | solution.py:22
  684.3 777.7 %all-reduce.23.cloned.1.call-start = ((), (), s32[]{:S(2)}) async-start(), calls=%async_computation.18 | async-start | bytes 5021696
  794.2 729.3 %all-reduce.25.cloned.1.call-start = ((), (), s32[]{:S(2)}) async-start(), calls=%async_computation.19 | async-start | bytes 5160960 | tf_op jit(solution)/shard_map/psum | solution.py:323
  1006.5 340.0 %copy-start.11 = (f32[256,3360]{0,1:T(8,128)S(1)}, f32[256,3360]{0,1:T(8,128)}, u32[]{:S(2)}) copy-start(f32[256,3360]{0,1:T(8,128)} %convert_element_type.222) | copy-start | bytes 10321924
  (47 other events, 253.7 us)
Sparse Core Ops, SparseCore 0:
  9.6 57.3 all-gather.4
  68.5 34.8 all-gather.6
  105.6 148.7 all-gather.8
  256.4 146.6 all-gather.10
  436.4 33.1 reduce-scatter.15
  554.0 67.1 reduce-scatter.13
  625.0 378.4 reduce-scatter.9
  1007.5 336.0 reduce-scatter.11
  1348.3 113.6 all-reduce.22
  1465.0 58.4 all-reduce.24
where the time goes:
time: 1540 us
  waiting for transfers between devices  1090 us (71%)
  matrix products  136 us (9%)
  other arithmetic  98.2 us (6%)
  blocking collectives  90.2 us (6%)
  local copies, waits for them, and re-layouts  83.9 us (5%)
  starting transfers between devices  22.6 us (1%)
  between operations  19.2 us (1%)
    reduce_scatter x1, waiting for transfers between devices, shards(): lax.psum_scatter(grad_wdown, 'cell', scatter_dimension=0, tiled=True)  337 us
    reduce_scatter x1, waiting for transfers between devices, shards(): lax.psum_scatter(grad_wup, 'cell', scatter_dimension=1, tiled=True)  188 us
    all_gather x1, waiting for transfers between devices, shards(): lax.all_gather(wdown, 'cell', axis=0, tiled=True)  139 us
    all_gather x1, waiting for transfers between devices, shards(): lax.all_gather(wup, 'cell', axis=1, tiled=True)  106 us
    unnamed x13, waiting for transfers between devices  86.9 us
    all_to_all x2, waiting for transfers between devices, sent_and_summed(): lax.all_to_all(parts, axis, split_axis=0, concat_axis=0, tiled=True)  73.3 us
    all_gather x1, waiting for transfers between devices, shards(): lax.all_gather(wqkv, 'seq', axis=0, tiled=True)  55.4 us
    psum x1, waiting for transfers between devices, shards(): lax.psum(cell_up.astype(jnp.bfloat16), 'seq').astype(jnp.float32)  54.1 us
  transfers between devices with their start and end apart: 15, of which 12 were waited for; matrix products, arithmetic and copies ran while one was open for 18% of the time, Pallas kernels for 0%

commit v1 on v0

v1 whole, which is shorter than its diff:
```python
import math

import jax
import jax.numpy as jnp
from jax import lax
from jax.sharding import Mesh
from jax.sharding import PartitionSpec as P

HEAD_DIM = 56


norm_eps = 1e-05


CELL = ("outer", "pair")
SEQ = ("far", "core")
WEIGHT = ("outer", "far", "core")


def swapped(x):
    return lax.ppermute(x, "pair", [(0, 1), (1, 0)])


def product(left, right):
    return jnp.dot(left, right, preferred_element_type=jnp.float32)


def left_inner(left, right):
    return lax.dot_general(
        left, right, (((0,), (0,)), ((), ())), preferred_element_type=jnp.float32
    )


def right_inner(left, right):
    return lax.dot_general(
        left, right, (((1,), (1,)), ((), ())), preferred_element_type=jnp.float32
    )


def norm_forward(hidden, gain, shift):
    centre = hidden - jnp.mean(hidden, axis=-1, keepdims=True)
    inverse = lax.rsqrt(jnp.mean(centre * centre, axis=-1, keepdims=True) + norm_eps)
    unit_rows = centre * inverse
    return (unit_rows * gain + shift, unit_rows, inverse)


def norm_backward(grad_rows, unit_rows, inverse, gain):
    scaled = grad_rows * gain
    inside = (
        scaled
        - jnp.mean(scaled, axis=-1, keepdims=True)
        - unit_rows * jnp.mean(scaled * unit_rows, axis=-1, keepdims=True)
    )
    return (inside * inverse, jnp.sum(grad_rows * unit_rows, axis=0), jnp.sum(grad_rows, axis=0))


def block_scores(queries, keys_used, first_row, length, score_scale):
    row_count = queries.shape[0]
    key_count = keys_used.shape[0]
    scores = (
        jnp.einsum("qhd,khd->hqk", queries, keys_used, preferred_element_type=jnp.float32)
        * score_scale
    )
    query_pos = first_row + lax.broadcasted_iota(jnp.int32, (row_count, key_count), 0)
    key_pos = lax.broadcasted_iota(jnp.int32, (row_count, key_count), 1)
    visible = (key_pos <= query_pos) & (key_pos < length)
    return jnp.where(visible[None], scores, -1e30)


def attend_forward(query_heads, key_heads, value_heads, length, row_block, score_scale):
    slot_count = query_heads.shape[0]
    outputs = []
    logsums = []
    for block_idx in range(slot_count // row_block):
        first_row = block_idx * row_block
        key_count = first_row + row_block
        scores = block_scores(
            query_heads[first_row:key_count], key_heads[:key_count], first_row, length, score_scale
        )
        highest = jnp.max(scores, axis=-1, keepdims=True)
        weights = jnp.exp(scores - highest)
        denominator = jnp.sum(weights, axis=-1, keepdims=True)
        prob_low = (weights / denominator).astype(jnp.bfloat16)
        outputs.append(
            jnp.einsum(
                "hqk,khd->qhd",
                prob_low,
                value_heads[:key_count],
                preferred_element_type=jnp.float32,
            )
        )
        logsums.append(highest + jnp.log(denominator))
    return (jnp.concatenate(outputs, axis=0), logsums)


def attend_backward(
    query_heads, key_heads, value_heads, grad_heads, logsums, length, row_block, score_scale
):
    slot_count = query_heads.shape[0]
    grad_query = []
    grad_key = jnp.zeros(key_heads.shape, jnp.float32)
    grad_value = jnp.zeros(value_heads.shape, jnp.float32)
    for block_idx in range(slot_count // row_block):
        first_row = block_idx * row_block
        key_count = first_row + row_block
        queries = query_heads[first_row:key_count]
        grads_here = grad_heads[first_row:key_count]
        scores = block_scores(queries, key_heads[:key_count], first_row, length, score_scale)
        prob_full = jnp.exp(scores - logsums[block_idx])
        prob_low = prob_full.astype(jnp.bfloat16)
        grad_prob = jnp.einsum(
            "qhd,khd->hqk", grads_here, value_heads[:key_count], preferred_element_type=jnp.float32
        )
        grad_value = grad_value.at[:key_count].add(
            jnp.einsum("hqk,qhd->khd", prob_low, grads_here, preferred_element_type=jnp.float32)
        )
        row_inner = jnp.sum(prob_full * grad_prob, axis=-1, keepdims=True)
        grad_score = (prob_full * (grad_prob - row_inner)).astype(jnp.bfloat16)
        grad_query.append(
            jnp.einsum(
                "hqk,khd->qhd",
                grad_score,
                key_heads[:key_count],
                preferred_element_type=jnp.float32,
            )
            * score_scale
        )
        grad_key = grad_key.at[:key_count].add(
            jnp.einsum("hqk,qhd->khd", grad_score, queries, preferred_element_type=jnp.float32)
            * score_scale
        )
    return (jnp.concatenate(grad_query, axis=0), grad_key, grad_value)


def shards(
    cells_in,
    dataset_ids,
    cell_lengths,
    table,
    wqkv,
    bq,
    bv,
    wout,
    bout,
    gain1,
    shift1,
    gain2,
    shift2,
    wup,
    bup,
    wdown,
    bdown,
    out_grad,
):
    low = jnp.bfloat16
    seq_count = lax.axis_size(SEQ)
    outer_count = lax.axis_size("outer")
    group = lax.axis_index(SEQ)
    pair = lax.axis_index("pair")
    local_rows = cells_in.shape[1]
    width = cells_in.shape[2]
    slot_count = local_rows * seq_count
    group_width = width // seq_count
    hidden = wup.shape[1]
    heads_here = group_width // HEAD_DIM
    row_block = min(512, slot_count)
    score_scale = 1.0 / math.sqrt(HEAD_DIM)
    length = cell_lengths[0]

    dataset_pick = (
        lax.broadcasted_iota(jnp.int32, (1, table.shape[0]), 1) == dataset_ids[0]
    ).astype(jnp.float32)
    table_row = jnp.dot(
        dataset_pick, table, precision=lax.Precision.HIGHEST, preferred_element_type=jnp.float32
    )
    resid_in = cells_in[0].astype(jnp.float32) + table_row
    normed1, unit1, inverse1 = norm_forward(resid_in, gain1, shift1)
    normed1_all = lax.all_gather(normed1.astype(low), SEQ, axis=0, tiled=True)
    group_weights = lax.all_to_all(
        wqkv.reshape(wqkv.shape[0], 3, seq_count, group_width),
        SEQ,
        split_axis=2,
        concat_axis=0,
        tiled=True,
    ).reshape(width, 3 * group_width)
    wout_full = lax.all_gather(wout, SEQ, axis=0, tiled=True)

    own_part = jnp.concatenate([wup.T, wdown], axis=0)
    part_rows = own_part.shape[0] // seq_count
    own_part = lax.dynamic_slice_in_dim(own_part, group * part_rows, part_rows, axis=0)
    ff_weights = lax.all_gather(own_part, WEIGHT, axis=0, tiled=True)
    ff_weights = ff_weights.reshape(outer_count, 2, hidden, width)
    wup_rows = ff_weights[:, 0].reshape(outer_count * hidden, width)
    wdown_rows = ff_weights[:, 1].reshape(outer_count * hidden, width)
    bup_here = lax.dynamic_index_in_dim(
        bup.reshape(outer_count, 2, hidden), pair, axis=1, keepdims=False
    ).reshape(-1)

    grad_out = out_grad[0]
    grad_out_both = jnp.concatenate([grad_out, swapped(grad_out)], axis=0)

    bias_here = lax.dynamic_slice_in_dim(
        jnp.stack([bq, jnp.zeros_like(bq), bv]), group * group_width, group_width, axis=1
    )
    qkv_heads = (product(normed1_all, group_weights) + bias_here.reshape(-1)).astype(low)
    query_heads, key_heads, value_heads = (
        qkv_heads[:, third * group_width : (third + 1) * group_width].reshape(
            slot_count, heads_here, HEAD_DIM
        )
        for third in range(3)
    )
    context, logsums = attend_forward(
        query_heads, key_heads, value_heads, length, row_block, score_scale
    )
    context_low = context.astype(low).reshape(slot_count, 1, group_width)
    context_rows = lax.all_to_all(
        context_low, SEQ, split_axis=0, concat_axis=1, tiled=True
    ).reshape(local_rows, width)
    resid_mid = resid_in + product(context_rows, wout_full) + bout
    normed2, unit2, inverse2 = norm_forward(resid_mid, gain2, shift2)
    normed2_low = normed2.astype(low)

    normed2_both = jnp.concatenate([normed2_low, swapped(normed2_low)], axis=0)
    up_rows = right_inner(normed2_both, wup_rows) + bup_here
    act_low = jax.nn.gelu(up_rows, approximate=True).astype(low)
    down_both = product(act_low, wdown_rows)
    down_here = down_both[:local_rows] + swapped(down_both[local_rows:].astype(low)).astype(
        jnp.float32
    )
    cells_out = (resid_mid + down_here + bdown).astype(low)[None]
    grad_rows = grad_out.astype(jnp.float32)
    grad_bdown = jnp.sum(grad_rows, axis=0)
    grad_wdown = left_inner(act_low, grad_out_both)
    grad_act = right_inner(grad_out_both, wdown_rows)
    gelu_pull = jax.vjp(lambda values: jax.nn.gelu(values, approximate=True), up_rows)[1]
    grad_up_low = gelu_pull(grad_act)[0].astype(low)
    grad_bup = jnp.sum(grad_up_low.astype(jnp.float32), axis=0)
    grad_wup = left_inner(grad_up_low, normed2_both)
    grad_norm2_both = product(grad_up_low, wup_rows)
    grad_norm2 = grad_norm2_both[:local_rows] + swapped(
        grad_norm2_both[local_rows:].astype(low)
    ).astype(jnp.float32)
    ff_grads = jnp.stack(
        [
            grad_wup.astype(low).reshape(outer_count, hidden, width),
            grad_wdown.astype(low).reshape(outer_count, hidden, width),
        ],
        axis=1,
    ).reshape(outer_count * 2 * hidden, width)
    ff_part = lax.psum_scatter(ff_grads, WEIGHT, scatter_dimension=0, tiled=True)
    ff_total = lax.all_gather(ff_part, SEQ, axis=0, tiled=True).astype(jnp.float32)
    total_up = ff_total[:hidden].T
    total_down = ff_total[hidden:]

    back_second, grad_gain2, grad_shift2 = norm_backward(grad_norm2, unit2, inverse2, gain2)
    grad_mid = grad_rows + back_second
    grad_mid_low = grad_mid.astype(low)
    grad_bout = jnp.sum(grad_mid_low.astype(jnp.float32), axis=0)
    grad_context = right_inner(grad_mid_low, wout_full).astype(low)
    grad_context_heads = lax.all_to_all(
        grad_context.reshape(local_rows, seq_count, group_width),
        SEQ,
        split_axis=1,
        concat_axis=0,
        tiled=True,
    ).reshape(slot_count, heads_here, HEAD_DIM)
    grad_wout = left_inner(context_rows, grad_mid_low)
    total_wout = lax.psum(
        lax.psum_scatter(grad_wout.astype(low), SEQ, scatter_dimension=0, tiled=True), CELL
    ).astype(jnp.float32)
    grad_query, grad_key, grad_value = attend_backward(
        query_heads,
        key_heads,
        value_heads,
        grad_context_heads,
        logsums,
        length,
        row_block,
        score_scale,
    )
    grad_qkv = jnp.concatenate(
        [part.reshape(slot_count, group_width) for part in (grad_query, grad_key, grad_value)],
        axis=1,
    ).astype(low)
    grad_norm1 = lax.psum_scatter(
        right_inner(grad_qkv, group_weights).astype(low), SEQ, scatter_dimension=0, tiled=True
    ).astype(jnp.float32)
    grad_wqkv = left_inner(normed1_all, grad_qkv).astype(low)
    grad_wqkv = lax.all_to_all(
        grad_wqkv.reshape(seq_count, group_width, 3 * group_width),
        SEQ,
        split_axis=0,
        concat_axis=0,
        tiled=True,
    )
    total_wqkv = lax.psum(grad_wqkv, CELL).astype(jnp.float32)
    total_wqkv = jnp.transpose(
        total_wqkv.reshape(seq_count, group_width, 3, group_width), (1, 2, 0, 3)
    ).reshape(group_width, 3 * width)
    grad_qkv_sums = jnp.sum(grad_qkv.astype(jnp.float32), axis=0)
    back_first, grad_gain1, grad_shift1 = norm_backward(grad_norm1, unit1, inverse1, gain1)
    grad_in = grad_mid + back_first
    cells_grad = grad_in.astype(low)[None]

    row_sums = jnp.stack(
        [
            jnp.sum(grad_in, axis=0),
            grad_bout,
            grad_gain1,
            grad_shift1,
            grad_gain2,
            grad_shift2,
            grad_bdown,
        ]
    )
    slot = (jnp.arange(2)[:, None] == pair).astype(jnp.float32)
    bup_slots = (slot * grad_bup.reshape(outer_count, 1, hidden)).reshape(seq_count, 1, -1)
    table_rows = jnp.transpose(dataset_pick) * row_sums[:1]
    own_group = (jnp.arange(seq_count)[:, None] == group).astype(jnp.float32)
    q_sums, v_sums = grad_qkv_sums[:group_width], grad_qkv_sums[2 * group_width :]
    small = jnp.concatenate(
        [
            jnp.concatenate([table_rows, row_sums[1:]])
            .reshape(-1, seq_count, group_width)
            .transpose(1, 0, 2)
            .reshape(seq_count, -1),
            own_group * q_sums,
            own_group * v_sums,
            bup_slots.reshape(seq_count, -1),
        ],
        axis=1,
    )
    small = lax.psum(small, ("outer", "pair", "far", "core"))
    small = lax.dynamic_index_in_dim(small, group, axis=0, keepdims=False)
    count = table.shape[0] + 6
    rows = small[: count * group_width].reshape(count, group_width)
    total_table = rows[: table.shape[0]]
    total_bout, total_gain1, total_shift1, total_gain2, total_shift2, total_bdown = rows[
        table.shape[0] :
    ]
    rest = small[count * group_width :]
    total_bq, total_bv, total_bup = (
        rest[:group_width],
        rest[group_width : 2 * group_width],
        rest[2 * group_width :],
    )
    return (
        cells_out,
        cells_grad,
        total_table,
        total_wqkv,
        total_bq,
        total_bv,
        total_wout,
        total_bout,
        total_gain1,
        total_shift1,
        total_gain2,
        total_shift2,
        total_up,
        total_bup,
        total_down,
        total_bdown,
    )


def solution(mesh):
    cells, seqs = mesh.devices.shape
    fine = Mesh(
        mesh.devices.reshape(cells // 2, 2, seqs // 2, 2), ("outer", "pair", "far", "core")
    )
    return jax.shard_map(
        shards,
        mesh=fine,
        in_specs=(
            P(CELL, SEQ, None),
            P(CELL),
            P(CELL),
            P(),
            P(SEQ, None),
            P(),
            P(),
            P(SEQ, None),
            P(),
            P(),
            P(),
            P(),
            P(),
            P(None, CELL),
            P(),
            P(CELL, None),
            P(),
            P(CELL, SEQ, None),
        ),
        out_specs=(
            P(CELL, SEQ, None),
            P(CELL, SEQ, None),
            P(None, SEQ),
            P(SEQ, None),
            P(SEQ),
            P(SEQ),
            P(SEQ, None),
            P(SEQ),
            P(SEQ),
            P(SEQ),
            P(SEQ),
            P(SEQ),
            P(None, CELL),
            P(SEQ),
            P(CELL, None),
            P(SEQ),
        ),
        check_vma=False,
    )
```

time: 1540 us -> 767 us (0.50)
  waiting for transfers between devices: 1090 us -> 509 us
  blocking collectives: 90.2 us -> 0 us
  other arithmetic: 98.2 us -> 42.2 us
  matrix products: 136 us -> 86.9 us
    reduce_scatter x2 -> x1, waiting for transfers between devices: 525 us -> 0.01 us  [shards(): lax.psum_scatter(right_inner(grad_qkv, group_weights).astype(low), SEQ, s...]
    all_gather x4, waiting for transfers between devices: 300 us -> 58.8 us  [the longest x1 37.4 us: shards(): ff_weights = lax.all_gather(own_part, WEIGHT, axis=0, tiled=True)]
    psum x1 -> x2, waiting for transfers between devices: 54.1 us -> 244 us  [the longest x1 129 us: shards(): small = lax.psum(small, ('outer', 'pair', 'far', 'core'))]
    convert_element_type x18 -> x6, other arithmetic: 61.7 us -> 8.04 us  [the longest x1 2.4 us: shards(): normed1_all = lax.all_gather(normed1.astype(low), SEQ, axis=0, tiled=True)]
    all_to_all x1 -> x0, blocking collectives: 39.4 us -> none  [shards(): lax.all_to_all(grad_qkv_heads.reshape(slot_count, 3, 1, group_width), 'se...]
    psum x1 -> x0, blocking collectives: 38.1 us -> none  [shards(): others = lax.psum((seq_parts[0],) + tuple(seq_parts[3:]), 'cell')]
    all_to_all x4 -> x3, waiting for transfers between devices: 112 us -> 77.4 us  [the longest x1 43.1 us: shards(): lax.all_to_all(wqkv.reshape(wqkv.shape[0], 3, seq_count, group_width), SE...]
    unnamed x126 -> x115, local copies, waits for them, and re-layouts: 43.3 us -> 12.1 us
  transfers between devices with their start and end apart: 15 -> 17, of which waited for: 12 -> 11; matrix products, arithmetic and copies ran while one was open for 18% -> 19% of each run, Pallas kernels for 0% -> 0%
where the time goes in v1:
time: 767 us; the launch traced here: 762 us
  waiting for transfers between devices  509 us (66%)
  matrix products  86.9 us (11%)
  local copies, waits for them, and re-layouts  84.6 us (11%)
  other arithmetic  42.2 us (6%)
  starting transfers between devices  22.3 us (3%)
  between operations  16.5 us (2%)
    psum x1, waiting for transfers between devices, shards(): small = lax.psum(small, ('outer', 'pair', 'far', 'core'))  129 us
    psum x1, waiting for transfers between devices, shards(): total_wqkv = lax.psum(grad_wqkv, CELL).astype(jnp.float32)  114 us
    unnamed x11, waiting for transfers between devices  99.2 us
    all_to_all x1, waiting for transfers between devices, shards(): lax.all_to_all(wqkv.reshape(wqkv.shape[0], 3, seq_count, group_width), SE...  43.1 us
    all_gather x1, waiting for transfers between devices, shards(): ff_weights = lax.all_gather(own_part, WEIGHT, axis=0, tiled=True)  37.4 us
    all_to_all x1, waiting for transfers between devices, shards(): lax.all_to_all(grad_wqkv.reshape(seq_count, group_width, 3 * group_width)...  26.5 us
    dot_general x4, matrix products, left_inner(): lax.dot_general(left, right, (((0,), (0,)), ((), ())), preferred_element_...  24.9 us
    ppermute x4, waiting for transfers between devices, swapped(): return lax.ppermute(x, 'pair', [(0, 1), (1, 0)])  21.5 us
  transfers between devices with their start and end apart: 17, of which 11 were waited for; matrix products, arithmetic and copies ran while one was open for 19% of the time, Pallas kernels for 0%

profile of v1, /device:TPU:0, one launch (start us, length us, event | category | flops | bytes accessed | tf_op | source)
XLA Modules:
  0.0 761.9 jit_solution(4957366146221555967)
XLA Ops:
  15.7 5.1 reshape.460
  20.8 5.0 copy.106
  33.5 43.1 %all-to-all-done = bf16[280,3,4,280]{0,3,1,2:T(8,128)(2,1)S(1)} async-done(((bf16[280,3,4,280]{0,3,1,2:T(8,128)(2,1)}), bf16[280,3,4,280]{0,3,1,2:T(8,128)(2,1)S(1)}, u32[]{:S(2)}, u32[]{:S(2)}) %all-to-all-start) | async-done | bytes 1881632 | tf_op jit(solution)/shard_map/all_to_all | solution.py:179
  111.6 7.7 %all-to-all-done.1 = bf16[4,2,35840]{2,1,0:T(2,128)(2,1)S(1)} async-done(((bf16[4,2,35840]{2,1,0:T(2,128)(2,1)}), bf16[4,2,35840]{2,1,0:T(2,128)(2,1)S(1)}, u32[]{:S(2)}, u32[]{:S(2)}) %all-to-all-start.1) | async-done | bytes 573472 | tf_op jit(solution)/shard_map/all_to_all | solution.py:216
  133.2 37.4 %all-gather.9.cloned.1.call-done = bf16[4480,1120]{1,0:T(8,128)(2,1)} async-done(((bf16[280,1120]{1,0:T(8,128)(2,1)}), bf16[4480,1120]{1,0:T(8,128)(2,1)}) %all-gather.9.cloned.1.call-update) | async-done | bytes 10035216 | tf_op jit(solution)/shard_map/all_gather | solution.py:191
  170.6 8.7 %fusion.83 = (bf16[4,1,560,1120]{3,2,1,0:T(8,128)(2,1)}, bf16[4,1,560,1120]{3,2,1,0:T(8,128)(2,1)}) fusion(bf16[4,2,560,1120]{3,2,1,0:T(8,128)(2,1)} %bitcast.137), kind=kLoop, calls=%fused_computation.165 | loop fusion | bytes 20070400 | tf_op jit(solution)/shard_map/slice | solution.py:193
  179.3 5.7 convolution_add_fusion
  185.1 6.2 convert_reduce_fusion
  199.5 10.7 %collective-permute-done.3 = bf16[256,1120]{0,1:T(8,128)(2,1)S(1)} collective-permute-done((bf16[256,1120]{0,1:T(8,128)(2,1)S(1)}, bf16[256,1120]{0,1:T(8,128)(2,1)S(1)}, u32[]{:S(2)}, u32[]{:S(2)}) %collective-permute-start.3) | collective-permute-done | bytes 573472 | tf_op jit(solution)/shard_map/ppermute | solution.py:21
  210.9 10.9 %collective-permute-done.1 = bf16[256,1120]{0,1:T(8,128)(2,1)S(1)} collective-permute-done((bf16[256,1120]{0,1:T(8,128)(2,1)S(1)}, bf16[256,1120]{0,1:T(8,128)(2,1)S(1)}, u32[]{:S(2)}, u32[]{:S(2)}) %collective-permute-start.1) | collective-permute-done | bytes 573472 | tf_op jit(solution)/shard_map/ppermute | solution.py:21
  229.2 9.0 %all-to-all-done.2 = bf16[256,4,280]{0,2,1:T(8,128)(2,1)S(1)} async-done(((bf16[256,4,280]{0,2,1:T(8,128)(2,1)}), bf16[256,4,280]{0,2,1:T(8,128)(2,1)S(1)}, u32[]{:S(2)}, u32[]{:S(2)}) %all-to-all-start.2) | async-done | bytes 573472 | tf_op jit(solution)/shard_map/all_to_all | solution.py:260
  254.9 7.1 multiply_reduce_fusion
  278.7 7.8 %convolution_convert_fusion.1 = bf16[2240,1120]{1,0:T(8,128)(2,1)} fusion(bf16[512,2240]{0,1:T(8,128)(2,1)} %copy-done.48, bf16[256,1120]{0,1:T(8,128)(2,1)} %collective-permute-done, bf16[256,1120]{0,1:T(8,128)(2,1)} %add_convert_fusion.1), kind=kOutput, calls=%fused_computation.1 | convolution fusion | flops 2573813760 | bytes 8458240 | tf_op jit(solution)/shard_map/dot_general | solution.py:29
  286.6 8.8 %convolution_convert_fusion = bf16[2240,1120]{1,0:T(8,128)(2,1)} fusion(bf16[256,1120]{0,1:T(8,128)(2,1)} %collective-permute-done.2, bf16[256,1120]{0,1:T(8,128)(2,1)S(1)} %bitcast.178, f32[512,2240]{0,1:T(8,128)} %copy-done.47), kind=kOutput, calls=%fused_computation | convolution fusion | flops 2584135680 | bytes 10752000 | tf_op jit(solution)/shard_map/dot_general | solution.py:29
  295.4 9.1 %pad_maximum_fusion = bf16[4,2,560,1120]{3,2,0,1:T(8,128)(2,1)} fusion(bf16[4,1,560,1120]{3,2,0,1:T(8,128)(2,1)} %bitcast.150, bf16[4,1,560,1120]{3,2,0,1:T(8,128)(2,1)} %bitcast.149), kind=kLoop, calls=%fused_computation.8 | loop fusion | flops 5017600 | bytes 20070400 | tf_op jit(solution)/shard_map/stack | solution.py:243
  304.5 8.7 %copy.120 = bf16[4,2,560,1120]{3,2,1,0:T(8,128)(2,1)} copy(bf16[4,2,560,1120]{3,2,0,1:T(8,128)(2,1)} %pad_maximum_fusion) | data formatting | bytes 20070400 | tf_op jit(solution)/shard_map/stack | solution.py:243
  314.3 5.8 convolution_convert_fusion.4
  336.3 26.5 %all-to-all-done.3 = bf16[4,280,840]{2,1,0:T(8,128)(2,1)} async-done(((bf16[4,280,840]{2,1,0:T(8,128)(2,1)}), bf16[4,280,840]{2,1,0:T(8,128)(2,1)}, u32[]{:S(2)}, u32[]{:S(2)}) %all-to-all-start.3) | async-done | bytes 1881632 | tf_op jit(solution)/shard_map/all_to_all | solution.py:289
  366.3 4.9 copy.119
  371.2 5.1 reshape.474
  376.3 98.4 %reduce-scatter.12.cloned.1.call-done = bf16[280,1120]{1,0:T(8,128)(2,1)} async-done(((bf16[4480,1120]{1,0:T(8,128)(2,1)}), bf16[280,1120]{1,0:T(8,128)(2,1)}) %reduce-scatter.12.cloned.1.call-update) | async-done | bytes 627216
  474.7 129.2 %all-reduce.8.cloned.1.call-done = f32[4,7840]{1,0:T(4,128)} async-done(((f32[4,7840]{1,0:T(4,128)}), f32[4,7840]{1,0:T(4,128)}) %all-reduce.8.cloned.1.call-update) | async-done | bytes 125456 | tf_op jit(solution)/shard_map/psum | solution.py:333
  608.5 114.3 %all-reduce.10.cloned.1.call-done = (bf16[280,3360]{1,0:T(8,128)(2,1)}, bf16[280,1120]{1,0:T(8,128)(2,1)}) async-done(((bf16[280,3360]{1,0:T(8,128)(2,1)}, bf16[280,1120]{1,0:T(8,128)(2,1)}), (bf16[280,3360]{1,0:T(8,128)(2,1)}, bf16[280,1120]{1,0:T(8,128)(2,1)})) %all-reduce.10.cloned.1.call-update) | async-done | bytes 2508816 | tf_op jit(solution)/shard_map/psum | solution.py:296
  727.4 21.5 %all-gather.11.cloned.1.call-done = bf16[1120,1120]{1,0:T(8,128)(2,1)} async-done(((bf16[280,1120]{1,0:T(8,128)(2,1)}), bf16[1120,1120]{1,0:T(8,128)(2,1)}) %all-gather.11.cloned.1.call-update) | async-done | bytes 2508816 | tf_op jit(solution)/shard_map/all_gather | solution.py:251
  (257 shorter events, 148.8 us)
Async XLA Ops:
  7.2 76.2 %all-gather.5.cloned.1.call-start = ((), (), s32[]{:S(2)}) async-start(), calls=%async_computation.7 | async-start | bytes 2867200 | tf_op jit(solution)/shard_map/all_gather | solution.py:178
  13.3 113.8 %all-gather.7.cloned.1.call-start = ((), (), s32[]{:S(2)}) async-start(), calls=%async_computation.8 | async-start | bytes 3225600 | tf_op jit(solution)/shard_map/all_gather | solution.py:186
  14.1 156.5 %all-gather.9.cloned.1.call-start = ((), (), s32[]{:S(2)}) async-start(), calls=%async_computation.9 | async-start | bytes 10967040 | tf_op jit(solution)/shard_map/all_gather | solution.py:191
  25.8 50.8 %all-to-all-start = ((bf16[280,3,4,280]{0,3,1,2:T(8,128)(2,1)}), bf16[280,3,4,280]{0,3,1,2:T(8,128)(2,1)S(1)}, u32[]{:S(2)}, u32[]{:S(2)}) async-start(bf16[280,3,4,280]{0,3,1,2:T(8,128)(2,1)} %copy.106), calls=%async_computation | async-start | bytes 5160960 | tf_op jit(solution)/shard_map/all_to_all | solution.py:179
  89.0 9.0 %copy-start.15 = (bf16[1024,280]{0,1:T(8,128)(2,1)}, bf16[1024,280]{0,1:T(8,128)(2,1)S(1)}, u32[]{:S(2)}) copy-start(bf16[1024,280]{0,1:T(8,128)(2,1)S(1)} %get-tuple-element.109) | copy-start | bytes 1720324
  102.4 9.0 %copy-start.38 = (f32[4480]{0:T(1024)S(1)}, f32[4480]{0:T(1024)}, u32[]{:S(2)}) copy-start(f32[4480]{0:T(1024)} %param.44) | copy-start | bytes 53764
  106.5 12.8 %all-to-all-start.1 = ((bf16[4,2,35840]{2,1,0:T(2,128)(2,1)}), bf16[4,2,35840]{2,1,0:T(2,128)(2,1)S(1)}, u32[]{:S(2)}, u32[]{:S(2)}) async-start(bf16[4,2,35840]{2,1,0:T(2,128)(2,1)} %reshape.495), calls=%async_computation.1 | async-start | bytes 1146880 | tf_op jit(solution)/shard_map/all_to_all | solution.py:216
  109.9 75.1 %collective-permute-start.2 = (bf16[256,1120]{0,1:T(8,128)(2,1)}, bf16[256,1120]{0,1:T(8,128)(2,1)}, u32[]{:S(2)}, u32[]{:S(2)}) collective-permute-start(bf16[256,1120]{0,1:T(8,128)(2,1)} %bitcast.176), channel_id=1, source_target_pairs={{0,4},{4,0},{1,5},{5,1},{2,6},{6,2},{3,7},{7,3},{8,12},{12,8},{9,1... | collective-permute-start | bytes 1720328 | tf_op jit(solution)/shard_map/ppermute | solution.py:21
  131.9 47.4 %collective-permute-start = (bf16[256,1120]{0,1:T(8,128)(2,1)}, bf16[256,1120]{0,1:T(8,128)(2,1)}, u32[]{:S(2)}, u32[]{:S(2)}) collective-permute-start(bf16[256,1120]{0,1:T(8,128)(2,1)} %add_convert_fusion.1), channel_id=1, source_target_pairs={{0,4},{4,0},{1,5},{5,1},{2,6},{6,2},{3,7},{7,3},{8,12},{12,8},{9,1... | collective-permute-start | bytes 1720328 | tf_op jit(solution)/shard_map/ppermute | solution.py:21
  179.3 11.9 %slice-start.5 = ((s8[5160960]{0:T(1024)(128)(4,1)}), s8[4194304]{0:T(1024)(128)(4,1)S(1)}, s32[]{:S(2)}) async-start(s8[5160960]{0:T(1024)(128)(4,1)} %bitcast.146), calls=%async_computation.21 | async-start | bytes 8388608
  185.0 10.8 %copy-start.47 = (f32[512,2240]{0,1:T(8,128)}, f32[512,2240]{0,1:T(8,128)S(1)}, u32[]{:S(2)}) copy-start(f32[512,2240]{0,1:T(8,128)S(1)} %convolution_add_fusion) | copy-start | bytes 13762564
  194.3 15.9 %collective-permute-start.3 = (bf16[256,1120]{0,1:T(8,128)(2,1)S(1)}, bf16[256,1120]{0,1:T(8,128)(2,1)S(1)}, u32[]{:S(2)}, u32[]{:S(2)}) collective-permute-start(bf16[256,1120]{0,1:T(8,128)(2,1)S(1)} %slice.282), channel_id=1, source_target_pairs={{0,4},{4,0},{1,5},{5,1},{2,6},{6,2},{3,7},{7,3},{8,12},{12,8},{9,1... | collective-permute-start | bytes 1720328 | tf_op jit(solution)/shard_map/ppermute | solution.py:21
  198.8 23.0 %copy-start.42 = (f32[1120]{0:T(1024)S(1)}, f32[1120]{0:T(1024)}, u32[]{:S(2)}) copy-start(f32[1120]{0:T(1024)} %param.46) | copy-start | bytes 13444
  198.9 22.9 %collective-permute-start.1 = (bf16[256,1120]{0,1:T(8,128)(2,1)S(1)}, bf16[256,1120]{0,1:T(8,128)(2,1)S(1)}, u32[]{:S(2)}, u32[]{:S(2)}) collective-permute-start(bf16[256,1120]{0,1:T(8,128)(2,1)S(1)} %slice.283), channel_id=1, source_target_pairs={{0,4},{4,0},{1,5},{5,1},{2,6},{6,2},{3,7},{7,3},{8,12},{12,8},{9,1... | collective-permute-start | bytes 1720328 | tf_op jit(solution)/shard_map/ppermute | solution.py:21
  225.4 12.8 %all-to-all-start.2 = ((bf16[256,4,280]{0,2,1:T(8,128)(2,1)}), bf16[256,4,280]{0,2,1:T(8,128)(2,1)S(1)}, u32[]{:S(2)}, u32[]{:S(2)}) async-start(bf16[256,4,280]{0,2,1:T(8,128)(2,1)} %bitcast.24), calls=%async_computation.2 | async-start | bytes 1146880 | tf_op jit(solution)/shard_map/all_to_all | solution.py:260
  228.9 101.6 %reduce-scatter.8.cloned.1.call-start = ((), (), s32[]{:S(2)}) async-start(), calls=%async_computation.10 | async-start | bytes 2867200 | tf_op jit(solution)/shard_map/reduce_scatter | solution.py:285
  250.4 11.7 %slice-start = ((s8[10485760]{0:T(1024)(128)(4,1)}), s8[2097152]{0:T(1024)(128)(4,1)S(1)}, s32[]{:S(2)}) async-start(s8[10485760]{0:T(1024)(128)(4,1)} %bitcast.132), calls=%async_computation.16 | async-start | bytes 4194304
  274.4 101.9 %reduce-scatter.10.cloned.1.call-start = ((), (), s32[]{:S(2)}) async-start(), calls=%async_computation.13 | async-start | bytes 3225600
  278.2 8.3 %copy-start.33 = (bf16[1,256,1120]{1,2,0:T(8,128)(2,1)S(1)}, bf16[1,256,1120]{1,2,0:T(8,128)(2,1)}, u32[]{:S(2)}) copy-start(bf16[1,256,1120]{1,2,0:T(8,128)(2,1)} %param.47) | copy-start | bytes 1720324
  278.2 196.5 %reduce-scatter.12.cloned.1.call-start = ((), (), s32[]{:S(2)}) async-start(), calls=%async_computation.14 | async-start | bytes 10967040
  324.1 38.7 %all-to-all-start.3 = ((bf16[4,280,840]{2,1,0:T(8,128)(2,1)}), bf16[4,280,840]{2,1,0:T(8,128)(2,1)}, u32[]{:S(2)}, u32[]{:S(2)}) async-start(bf16[4,280,840]{2,1,0:T(8,128)(2,1)} %bitcast.140), calls=%async_computation.4 | async-start | bytes 4014080 | tf_op jit(solution)/shard_map/all_to_all | solution.py:289
  328.7 275.2 %all-reduce.8.cloned.1.call-start = ((), (), s32[]{:S(2)}) async-start(), calls=%async_computation.11 | async-start | bytes 253952 | tf_op jit(solution)/shard_map/psum | solution.py:333
  336.3 386.6 %all-reduce.10.cloned.1.call-start = ((), (), s32[]{:S(2)}) async-start(), calls=%async_computation.15 | async-start | bytes 5160960 | tf_op jit(solution)/shard_map/psum | solution.py:296
  376.3 372.5 %all-gather.11.cloned.1.call-start = ((), (), s32[]{:S(2)}) async-start(), calls=%async_computation.12 | async-start | bytes 3225600 | tf_op jit(solution)/shard_map/all_gather | solution.py:251
  (49 other events, 200.8 us)
Sparse Core Ops, SparseCore 0:
  13.4 31.2 all-gather.4
  46.3 35.0 all-gather.6
  84.1 86.4 all-gather.8
  274.5 30.6 reduce-scatter.7
  308.2 43.8 reduce-scatter.9
  356.0 118.6 reduce-scatter.11
  480.8 123.0 all-reduce.7
  608.2 114.6 all-reduce.9
  724.4 24.3 all-gather.10
